TPU v7x, 128 devices: a whole 4x4x4 slice. The times are simulated.
128 devices in a mesh: dom: 32 (over z, y, core), sub: 4 (over x).
Axes of the slice: x: 4, y: 4, z: 4, core: 2. Of those that a mesh axis runs over, the one named last changes fastest.
Arguments:
- node_state: bfloat16 [64, 131072], P(None, ('dom', 'sub')), may hold values from -6 to 6
- edge_state: bfloat16 [64, 393216], P(None, ('dom', 'sub')), may hold values from -6 to 6
- senders: int32 [393216], P(('dom', 'sub')), may hold values from 0 to 2559, as said below
- receivers: int32 [393216], P(('dom', 'sub')), may hold values from 0 to 1023
- send_index: int32 [128, 12, 128], P(('dom', 'sub')), may hold values from -1 to 1023, as said below
- node_cotangent: bfloat16 [64, 131072], P(None, ('dom', 'sub')), may hold values from -6 to 6
- edge_cotangent: bfloat16 [64, 393216], P(None, ('dom', 'sub')), may hold values from -6 to 6
- edge_first: bfloat16 [192, 64], replicated, may hold values from -0.4375 to 0.4375
- edge_bias: float32 [64], replicated, may hold values from -3 to 3
- edge_second: bfloat16 [64, 64], replicated, may hold values from -0.75 to 0.75
- edge_gain: float32 [64], replicated, may hold values from 0.1 to 1.9
- edge_shift: float32 [64], replicated, may hold values from -3 to 3
- node_first: bfloat16 [128, 64], replicated, may hold values from -0.5 to 0.5
- node_bias: float32 [64], replicated, may hold values from -3 to 3
- node_second: bfloat16 [64, 64], replicated, may hold values from -0.75 to 0.75
- node_gain: float32 [64], replicated, may hold values from 0.1 to 1.9
Outputs:
- delta_state: bfloat16 [64, 131072], P(None, ('dom', 'sub'))
- delta_edges: bfloat16 [64, 393216], P(None, ('dom', 'sub'))
- delta_edgefirst: float32 [192, 64], replicated
- delta_edgebias: float32 [64], replicated
- delta_edgesecond: float32 [64, 64], replicated
- delta_edgegain: float32 [64], replicated
- delta_edgeshift: float32 [64], replicated
- delta_nodefirst: float32 [128, 64], replicated
- delta_nodebias: float32 [64], replicated
- delta_nodesecond: float32 [64, 64], replicated
- delta_nodegain: float32 [64], replicated
- delta_nodeshift: float32 [64], replicated
Inputs may be any that keep to these rules, and one draw needn't show every extreme that they name: `send_index`: block k = o * 4 + t of partition p = d * 4 + s lists own cells that p sends to the partition at dom index d + o - 1 and sub index t: live entries first, then -1. Blocks towards a dom index outside the mesh, and block 4 + s, hold only -1; every other block holds 32 to 128 live entries. Some partition receives a full block from every partition that sends to it. `senders`: an entry below 1024 is an own cell. An entry 1024 + k * 128 + j with k = o * 4 + u names ghost slot j of block k: the j-th entry of block o * 4 + s of the partition at dom index d + 1 - o and sub index u, and that entry is live.
All inputs are finite; a program needn't handle non-finite values.
Results may differ from a plain program's by a relative error of at most 0.0095.
Values may be sent and summed in bfloat16 or wider, within the bound.
A program may use at most 64 MiB of HBM per device.

v0:
```python
import math
import jax
import jax.numpy as jnp
from jax import lax
from jax.sharding import Mesh
from jax.sharding import PartitionSpec as P

DOM = ("dom_0", "dom_1", "dom_2")
DOM_SUB = ("dom_0", "dom_1", "dom_2", "sub")
EPSILON = 1e-05


def from_behind(value, axis, steps):
    count = lax.axis_size(axis)
    first, last = (max(0, -steps), min(count, count - steps))
    return lax.ppermute(value, axis, [(source, source + steps) for source in range(first, last)])


def in_blocks(array, dim, peers):
    before, after = (array.shape[:dim], array.shape[dim + 1 :])
    return jnp.moveaxis(array.reshape(*before, peers, -1, *after), dim, 0)


def sum_at_owner(array, axis, dim):
    peers = lax.axis_size(axis)
    tiles = lax.all_to_all(in_blocks(array, dim, peers), axis, 0, 0, tiled=True)
    return jnp.sum(tiles, axis=0)


def sum_in_two_steps(array, axes, dim):
    far, near = axes
    own = sum_at_owner(in_blocks(array, dim, lax.axis_size(far)), near, dim + 1)
    return jnp.sum(lax.all_to_all(own, far, 0, 0, tiled=True), axis=0)


def padded_to(lines, peers):
    spare = -len(lines) % peers
    return jnp.pad(lines, [(0, spare)] + [(0, 0)] * (lines.ndim - 1))


def copy_for_each(array, axis):
    peers = lax.axis_size(axis)
    return lax.all_to_all(
        jnp.broadcast_to(array[None], (peers, *array.shape)), axis, 0, 0, tiled=True
    )


def in_order(tiles, dim):
    tiles = jnp.moveaxis(tiles, 0, dim)
    shape = tiles.shape
    return tiles.reshape(*shape[:dim], shape[dim] * shape[dim + 1], *shape[dim + 2 :])


def whole_of(array, axes, dim):
    far, near = axes
    tiles = copy_for_each(copy_for_each(array, far), near)
    return in_order(tiles.swapaxes(0, 1).reshape(-1, *array.shape), dim)


def total_of(array, axes):
    own = sum_in_two_steps(
        padded_to(array, lax.axis_size(axes[0]) * lax.axis_size(axes[1])), axes, 0
    )
    whole = whole_of(own, axes, 0)
    return whole[: len(array)].reshape(array.shape)


def packed_total(arrays, axis):
    ends = [0]
    for a in arrays:
        ends.append(ends[-1] + a.size)
    running = total_of(jnp.concatenate([a.ravel() for a in arrays]), axis)
    return tuple((running[b:e].reshape(a.shape) for a, b, e in zip(arrays, ends, ends[1:])))


def contract_first(first_operand, second_operand):
    return lax.dot_general(
        first_operand, second_operand, (((0,), (0,)), ((), ())), preferred_element_type=jnp.float32
    )


def contract_last(first_operand, second_operand):
    return lax.dot_general(
        first_operand, second_operand, (((1,), (1,)), ((), ())), preferred_element_type=jnp.float32
    )


def sigmoid_linear(values):
    return values * jax.nn.sigmoid(values)


def sigmoid_slope(values):
    logistic = jax.nn.sigmoid(values)
    return logistic * (1.0 + values * (1.0 - logistic))


def standardize(values):
    centered = values - jnp.mean(values, axis=0, keepdims=True)
    spread = lax.rsqrt(jnp.mean(centered * centered, axis=0, keepdims=True) + EPSILON)
    return (centered * spread, spread)


def normalize_back(upstream, scaled, spread, gain_vector):
    gain_delta = jnp.sum(upstream * scaled, axis=1)
    shift_delta = jnp.sum(upstream, axis=1)
    weighted = upstream * gain_vector[:, None]
    result = spread * (
        weighted
        - jnp.mean(weighted, axis=0, keepdims=True)
        - scaled * jnp.mean(weighted * scaled, axis=0, keepdims=True)
    )
    return (result, gain_delta, shift_delta)


def block_sizes(count, width):
    step = math.gcd(count, 512)
    piece = math.gcd(width, 2048)
    return (step, piece)


def pick_precision(values):
    if values.dtype == jnp.float32:
        return lax.Precision.DEFAULT
    return None


def column_gather(table, index):
    rows, width = table.shape
    count = index.shape[0]
    step, piece = block_sizes(count, width)
    blocks = index.reshape(count // step, step)
    precision = pick_precision(table)

    def one_block(number, result):
        chosen = lax.dynamic_index_in_dim(blocks, number, 0, keepdims=False)
        total = jnp.zeros((rows, step), jnp.float32)
        for begin in range(0, width, piece):
            columns = lax.iota(jnp.int32, piece) + begin
            selector = (columns[:, None] == chosen[None, :]).astype(table.dtype)
            total = total + jnp.dot(
                table[:, begin : begin + piece],
                selector,
                precision=precision,
                preferred_element_type=jnp.float32,
            )
        return lax.dynamic_update_slice_in_dim(result, total.astype(table.dtype), number * step, 1)

    return lax.fori_loop(0, count // step, one_block, jnp.zeros((rows, count), table.dtype))


def column_scatter(values, index, width):
    rows, count = values.shape
    step, piece = block_sizes(count, width)
    blocks = index.reshape(count // step, step)
    precision = pick_precision(values)

    def one_block(number, result):
        chosen = lax.dynamic_index_in_dim(blocks, number, 0, keepdims=False)
        portion = lax.dynamic_slice_in_dim(values, number * step, step, 1)
        pieces = []
        for begin in range(0, width, piece):
            columns = lax.iota(jnp.int32, piece) + begin
            selector = (chosen[:, None] == columns[None, :]).astype(values.dtype)
            pieces.append(
                jnp.dot(portion, selector, precision=precision, preferred_element_type=jnp.float32)
            )
        return result + jnp.concatenate(pieces, axis=1)

    return lax.fori_loop(0, count // step, one_block, jnp.zeros((rows, width), jnp.float32))


def local_backward(
    extended,
    node_state,
    edge_state,
    senders,
    receivers,
    node_cotangent,
    edge_cotangent,
    edge_first,
    edge_bias,
    edge_second,
    edge_gain,
    edge_shift,
    node_first,
    node_bias,
    node_second,
    node_gain,
):
    features, cell_count = node_state.shape
    sender_rows = column_gather(extended, senders)
    receiver_rows = column_gather(node_state, receivers)
    stacked = jnp.concatenate([sender_rows, receiver_rows, edge_state], axis=0)
    edge_linear = contract_first(edge_first, stacked) + edge_bias[:, None]
    edge_active = sigmoid_linear(edge_linear).astype(jnp.bfloat16)
    edge_output = contract_first(edge_second, edge_active)
    edge_scaled, edge_spread = standardize(edge_output)
    message = (edge_scaled * edge_gain[:, None] + edge_shift[:, None]).astype(jnp.bfloat16)
    summed = column_scatter(message, receivers, cell_count)
    node_input = jnp.concatenate([node_state, summed.astype(jnp.bfloat16)], axis=0)
    node_linear = contract_first(node_first, node_input) + node_bias[:, None]
    node_active = sigmoid_linear(node_linear).astype(jnp.bfloat16)
    node_output = contract_first(node_second, node_active)
    node_scaled, node_spread = standardize(node_output)
    upstream = node_cotangent.astype(jnp.float32)
    node_delta, nodegain_delta, nodeshift_delta = normalize_back(
        upstream, node_scaled, node_spread, node_gain
    )
    node_delta = node_delta.astype(jnp.bfloat16)
    nodesecond_delta = contract_last(node_active, node_delta)
    node_hidden = jnp.dot(
        node_second, node_delta, preferred_element_type=jnp.float32
    ) * sigmoid_slope(node_linear)
    nodebias_delta = jnp.sum(node_hidden, axis=1)
    node_hidden = node_hidden.astype(jnp.bfloat16)
    nodefirst_delta = contract_last(node_input, node_hidden)
    node_back = jnp.dot(node_first, node_hidden, preferred_element_type=jnp.float32)
    message_delta = edge_cotangent.astype(jnp.float32) + column_gather(
        node_back[features:], receivers
    )
    edge_delta, edgegain_delta, edgeshift_delta = normalize_back(
        message_delta, edge_scaled, edge_spread, edge_gain
    )
    edge_delta = edge_delta.astype(jnp.bfloat16)
    edgesecond_delta = contract_last(edge_active, edge_delta)
    edge_hidden = jnp.dot(
        edge_second, edge_delta, preferred_element_type=jnp.float32
    ) * sigmoid_slope(edge_linear)
    edgebias_delta = jnp.sum(edge_hidden, axis=1)
    edge_hidden = edge_hidden.astype(jnp.bfloat16)
    edgefirst_delta = contract_last(stacked, edge_hidden)
    edge_back = jnp.dot(edge_first, edge_hidden, preferred_element_type=jnp.float32)
    edge_result = (edge_cotangent.astype(jnp.float32) + edge_back[2 * features :]).astype(
        jnp.bfloat16
    )
    scattered = column_scatter(edge_back[:features], senders, extended.shape[1])
    local_delta = (
        scattered[:, :cell_count]
        + column_scatter(edge_back[features : 2 * features], receivers, cell_count)
        + node_back[:features]
        + upstream
    )
    ghost_delta = scattered[:, cell_count:]
    partials = (
        edgefirst_delta,
        edgebias_delta,
        edgesecond_delta,
        edgegain_delta,
        edgeshift_delta,
        nodefirst_delta,
        nodebias_delta,
        nodesecond_delta,
        nodegain_delta,
        nodeshift_delta,
    )
    return (local_delta, ghost_delta, edge_result, partials)


def on_device(
    node_state,
    edge_state,
    senders,
    receivers,
    send_index,
    node_cotangent,
    edge_cotangent,
    edge_first,
    edge_bias,
    edge_second,
    edge_gain,
    edge_shift,
    node_first,
    node_bias,
    node_second,
    node_gain,
):
    features, cell_count = node_state.shape
    sub_count = lax.axis_size("sub")
    peer_count = 3 * sub_count
    halo_width = send_index.shape[2]
    index_rows = send_index.reshape(peer_count, halo_width)
    live_slots = index_rows >= 0
    safe_index = jnp.where(live_slots, index_rows, 0).reshape(-1)
    picked = column_gather(node_state, safe_index).reshape(features, peer_count, halo_width)
    outgoing = jnp.where(live_slots[None], picked, jnp.zeros_like(picked))
    blocks = outgoing.reshape(features, 3, sub_count, halo_width)
    across = lax.all_to_all(blocks, "sub", split_axis=2, concat_axis=2, tiled=True)
    upper = from_behind(across[:, 0], DOM, -1)
    lower = from_behind(across[:, 2], DOM, 1)
    ghost_rows = jnp.stack([upper, across[:, 1], lower], axis=1).reshape(
        features, peer_count, halo_width
    )
    extended = jnp.concatenate([node_state, ghost_rows.reshape(features, -1)], axis=1)
    local_delta, ghost_delta, edge_result, partials = local_backward(
        extended,
        node_state,
        edge_state,
        senders,
        receivers,
        node_cotangent,
        edge_cotangent,
        edge_first,
        edge_bias,
        edge_second,
        edge_gain,
        edge_shift,
        node_first,
        node_bias,
        node_second,
        node_gain,
    )
    ghost_delta = ghost_delta.reshape(features, peer_count, halo_width)
    grouped = ghost_delta.reshape(features, 3, sub_count, halo_width)
    further = from_behind(grouped[:, 0].astype(jnp.bfloat16), DOM, 1).astype(jnp.float32)
    nearer = from_behind(grouped[:, 2].astype(jnp.bfloat16), DOM, -1).astype(jnp.float32)
    regrouped = jnp.stack([further, grouped[:, 1], nearer], axis=1)
    returned = (
        lax.all_to_all(
            regrouped.astype(jnp.bfloat16), "sub", split_axis=2, concat_axis=2, tiled=True
        )
        .astype(regrouped.dtype)
        .reshape(features, peer_count, halo_width)
    )
    masked = jnp.where(live_slots[None], returned, jnp.zeros_like(returned)).reshape(features, -1)
    local_delta = local_delta + column_scatter(masked, safe_index, cell_count)
    totals = packed_total(
        (
            partials[0],
            partials[1],
            partials[2],
            partials[3],
            partials[4],
            partials[5],
            partials[6],
            partials[7],
            partials[8],
            partials[9],
        ),
        (("dom_0", "dom_1"), ("dom_2", "sub")),
    )
    faces_total = edge_state.shape[1] * lax.axis_size(DOM) * sub_count
    factor = 1.0 / math.sqrt(faces_total)
    (
        edgefirst_sum,
        edgebias_sum,
        edgesecond_sum,
        edgegain_sum,
        edgeshift_sum,
        nodefirst_sum,
        nodebias_sum,
        nodesecond_sum,
        nodegain_sum,
        nodeshift_sum,
    ) = totals
    return (
        local_delta.astype(jnp.bfloat16),
        edge_result,
        edgefirst_sum * factor,
        edgebias_sum * factor,
        edgesecond_sum * factor,
        edgegain_sum * factor,
        edgeshift_sum * factor,
        nodefirst_sum * factor,
        nodebias_sum * factor,
        nodesecond_sum * factor,
        nodegain_sum * factor,
        nodeshift_sum * factor,
    )


def solution(mesh):
    split = Mesh(
        mesh.devices.reshape(4, 4, 2, mesh.shape["sub"]), ("dom_0", "dom_1", "dom_2", "sub")
    )
    in_specs = (
        P(None, DOM_SUB),
        P(None, DOM_SUB),
        P(DOM_SUB),
        P(DOM_SUB),
        P(DOM_SUB, None, None),
        P(None, DOM_SUB),
        P(None, DOM_SUB),
        P(),
        P(),
        P(),
        P(),
        P(),
        P(),
        P(),
        P(),
        P(),
    )
    out_specs = (
        P(None, DOM_SUB),
        P(None, DOM_SUB),
        P(),
        P(),
        P(),
        P(),
        P(),
        P(),
        P(),
        P(),
        P(),
        P(),
    )
    return jax.shard_map(
        on_device, mesh=split, in_specs=in_specs, out_specs=out_specs, check_vma=False
    )
```

profile of v0, /device:TPU:1, one launch (start us, length us, event | category | flops | bytes accessed | tf_op | source)
XLA Modules:
  0.0 186.6 jit_solution(18048583148470305072)
XLA Ops:
  2.2 4.2 %while.108 = (s32[]{:T(128)}, bf16[64,1536]{1,0:T(8,128)(2,1)S(1)}, s32[3,512]{1,0:T(4,128)S(1)}, bf16[64,1024]{1,0:T(8,128)(2,1)}, s32[]{:T(128)}, /*index=5*/s32[]{:T(128)}, s32[]{:T(128)}, s32[]{:T(128)}) while((s32[]{:T(128)}, bf16[64,1536]{1,0:T(8,128)(2,1)S(1)}, s32[3,512]{1,0:T(4,128)S(1)}, bf16[64,1024]{1,0:T(8,128)(2,1)}, s32[]{:T(128)}, ...), condition=%wide.region_1.2_spmd, body=%wide.region_0.1_spmd.sunk | while | flops 67665928 | bytes 202891 | solution.py:148
  2.2 1.4 fusion.170
  3.6 1.4 fusion.170
  5.0 1.4 fusion.170
  7.9 4.8 %all-to-all-start = ((bf16[64,3,4,128]{3,0,1,2:T(8,128)(2,1)}), bf16[64,3,4,128]{3,0,1,2:T(8,128)(2,1)S(1)}, u32[]{:S(2)}, u32[]{:S(2)}) async-start(bf16[64,3,4,128]{3,0,1,2:T(8,128)(2,1)} %copy.70), calls=%async_computation | async-start | bytes 393216 | tf_op jit(solution)/shard_map/all_to_all | solution.py:287
  12.7 5.2 %all-to-all-done = bf16[64,3,4,128]{3,0,1,2:T(8,128)(2,1)S(1)} async-done(((bf16[64,3,4,128]{3,0,1,2:T(8,128)(2,1)}), bf16[64,3,4,128]{3,0,1,2:T(8,128)(2,1)S(1)}, u32[]{:S(2)}, u32[]{:S(2)}) %all-to-all-start) | async-done | bytes 196640 | tf_op jit(solution)/shard_map/all_to_all | solution.py:287
  17.9 5.2 %collective-permute-start.1 = (bf16[64,4,128]{2,0,1:T(8,128)(2,1)S(1)}, bf16[64,4,128]{2,0,1:T(8,128)(2,1)S(1)}, u32[]{:S(2)}, u32[]{:S(2)}) collective-permute-start(bf16[64,4,128]{2,0,1:T(8,128)(2,1)S(1)} %get-tuple-element.869), channel_id=1, source_target_pairs={{0,4},{4,8},{8,12},{12,16},{16,20},{20,24},{24,28},{28,32},{32,36}... | collective-permute-start | bytes 196616 | tf_op jit(solution)/shard_map/ppermute | solution.py:16
  23.1 1.9 %collective-permute-start = (bf16[64,4,128]{2,0,1:T(8,128)(2,1)S(1)}, bf16[64,4,128]{2,0,1:T(8,128)(2,1)S(1)}, u32[]{:S(2)}, u32[]{:S(2)}) collective-permute-start(bf16[64,4,128]{2,0,1:T(8,128)(2,1)S(1)} %get-tuple-element.868), channel_id=1, source_target_pairs={{4,0},{8,4},{12,8},{16,12},{20,16},{24,20},{28,24},{32,28},{36,32}... | collective-permute-start | bytes 196616 | tf_op jit(solution)/shard_map/ppermute | solution.py:16
  25.1 3.0 %while.110 = (s32[]{:T(128)}, bf16[64,3072]{1,0:T(8,128)(2,1)S(1)}, s32[6,512]{1,0:T(8,128)S(1)}, bf16[64,1024]{1,0:T(8,128)(2,1)S(1)}, s32[]{:T(128)}, /*index=5*/s32[]{:T(128)}, s32[]{:T(128)}, s32[]{:T(128)}) while((s32[]{:T(128)}, bf16[64,3072]{1,0:T(8,128)(2,1)S(1)}, s32[6,512]{1,0:T(8,128)S(1)}, bf16[64,1024]{1,0:T(8,128)(2,1)S(1)}, ...), condition=%wide.region_5.6_spmd, body=%wide.region_4.5_spmd.sunk | while | flops 67665928 | bytes 202891 | solution.py:148
  29.0 11.0 %while.109 = (s32[]{:T(128)}, bf16[64,3072]{1,0:T(8,128)(2,1)S(1)}, s32[6,512]{1,0:T(8,128)S(1)}, bf16[64,1024]{1,0:T(8,128)(2,1)S(1)}, bf16[64,1536]{1,0:T(8,12...) while((s32[]{:T(128)}, bf16[64,3072]{1,0:T(8,128)(2,1)S(1)}, s32[6,512]{1,0:T(8,128)S(1)}, ...), condition=%wide.region_3.4_spmd, body=%wide.region_2.3_spmd.sunk | while | flops 169248768 | bytes 1472659 | solution.py:148
  40.8 1.3 multiply_convert_fusion
  42.7 3.7 %while.112 = (s32[]{:T(128)}, f32[64,1024]{1,0:T(8,128)S(1)}, bf16[64,3072]{1,0:T(8,128)(2,1)S(1)}, s32[6,512]{1,0:T(8,128)S(1)}, s32[]{:T(128)}, /*index=5*/s32[]{:T(128)}, s32[]{:T(128)}, s32[]{:T(128)}) while((s32[]{:T(128)}, f32[64,1024]{1,0:T(8,128)S(1)}, bf16[64,3072]{1,0:T(8,128)(2,1)S(1)}, s32[6,512]{1,0:T(8,128)S(1)}, ...), condition=%wide.region_9.10_spmd.clone, body=%wide.region_8.9_spmd.clone.sunk | while | flops 67764232 | bytes 596117 | solution.py:169
  51.6 3.0 %while.111 = (s32[]{:T(128)}, f32[64,3072]{1,0:T(8,128)S(1)}, s32[6,512]{1,0:T(8,128)S(1)}, bf16[64,1024]{1,0:T(8,128)(2,1)S(1)}, s32[]{:T(128)}, /*index=5*/s32[]{:T(128)}, s32[]{:T(128)}, s32[]{:T(128)}) while((s32[]{:T(128)}, f32[64,3072]{1,0:T(8,128)S(1)}, s32[6,512]{1,0:T(8,128)S(1)}, bf16[64,1024]{1,0:T(8,128)(2,1)S(1)}, s32[]{:T(128)}, ...), condition=%wide.region_15.16_spmd, body=%wide.region_14.15_spmd.sunk | while | flops 67633160 | bytes 268427 | solution.py:148
  54.7 1.4 fusion.85
  59.5 1.5 reshape.185
  61.0 1.5 reshape.184
  62.5 1.4 reshape.183
  64.6 1.6 concatenate.18
  66.2 1.9 %reshape_reshape.16 = f32[16,8,227]{2,1,0:T(8,128)} reshape(f32[29056]{0:T(1024)} %concatenate.18) | data formatting | bytes 232448 | tf_op jit(solution)/shard_map/reshape;reshape | solution.py:21
  68.1 1.6 copy.81
  69.6 3.9 %all-to-all-start.2 = ((f32[8,16,227]{2,1,0:T(8,128)}), f32[8,16,227]{2,1,0:T(8,128)}, u32[]{:S(2)}, u32[]{:S(2)}) async-start(f32[8,16,227]{2,1,0:T(8,128)} %copy.81), calls=%async_computation.2 | async-start | bytes 262144 | tf_op jit(solution)/shard_map/all_to_all | solution.py:26
  74.6 42.4 %while.113 = (s32[]{:T(128)}, f32[64,2560]{1,0:T(8,128)S(1)}, bf16[64,3072]{1,0:T(8,128)(2,1)}, s32[6,512]{1,0:T(8,128)}, s32[]{:T(128)}, /*index=5*/s32[]{:T(128)}, s32[]{:T(128)}, s32[]{:T(128)}) while((s32[]{:T(128)}, f32[64,2560]{1,0:T(8,128)S(1)}, bf16[64,3072]{1,0:T(8,128)(2,1)}, s32[6,512]{1,0:T(8,128)}, s32[]{:T(128)}, ...), condition=%wide.region_19.20_spmd.clone, body=%wide.region_18.19_spmd.clone.sunk | while | flops 169412608 | bytes 2980005 | solution.py:169
  77.8 1.2 convolution_dynamic-update-slice_fusion.12
  80.2 1.2 convolution_dynamic-update-slice_fusion.14
  83.6 1.2 convolution_dynamic-update-slice_fusion.11
  86.1 1.2 convolution_dynamic-update-slice_fusion.13
  90.7 1.2 convolution_dynamic-update-slice_fusion.11
  93.1 1.2 convolution_dynamic-update-slice_fusion.13
  94.3 1.2 convolution_dynamic-update-slice_fusion.14
  99.0 1.2 convolution_dynamic-update-slice_fusion.12
  107.3 1.2 convolution_dynamic-update-slice_fusion.13
  117.2 3.2 %collective-permute-start.2 = (bf16[64,4,128]{2,1,0:T(4,128)(2,1)S(1)}, bf16[64,4,128]{2,1,0:T(4,128)(2,1)S(1)}, u32[]{:S(2)}, u32[]{:S(2)}) collective-permute-start(bf16[64,4,128]{2,1,0:T(4,128)(2,1)S(1)} %get-tuple-element.865), channel_id=1, source_target_pairs={{0,4},{4,8},{8,12},{12,16},{16,20},{20,24},{24,28},{28,32},{32,36}... | collective-permute-start | bytes 196616 | tf_op jit(solution)/shard_map/ppermute | solution.py:16
  120.4 1.9 %collective-permute-start.3 = (bf16[64,4,128]{2,1,0:T(4,128)(2,1)S(1)}, bf16[64,4,128]{2,1,0:T(4,128)(2,1)S(1)}, u32[]{:S(2)}, u32[]{:S(2)}) collective-permute-start(bf16[64,4,128]{2,1,0:T(4,128)(2,1)S(1)} %get-tuple-element.866), channel_id=1, source_target_pairs={{4,0},{8,4},{12,8},{16,12},{20,16},{24,20},{28,24},{32,28},{36,32}... | collective-permute-start | bytes 196616 | tf_op jit(solution)/shard_map/ppermute | solution.py:16
  123.9 9.2 %all-to-all-start.3 = ((f32[16,1,227]{2,1,0:T(1,128)}), f32[16,1,227]{2,1,0:T(1,128)S(1)}, u32[]{:S(2)}, u32[]{:S(2)}) async-start(f32[16,1,227]{2,1,0:T(1,128)} %all_to_all.25), calls=%async_computation.3 | async-start | bytes 32768 | tf_op jit(solution)/shard_map/all_to_all | solution.py:33
  133.1 13.6 %while.114 = (s32[]{:T(128)}, f32[64,1024]{1,0:T(8,128)}, bf16[64,3072]{1,0:T(8,128)(2,1)}, s32[6,512]{1,0:T(8,128)S(1)}, s32[]{:T(128)}, /*index=5*/s32[]{:T(128)}, s32[]{:T(128)}, s32[]{:T(128)}) while((s32[]{:T(128)}, f32[64,1024]{1,0:T(8,128)}, bf16[64,3072]{1,0:T(8,128)(2,1)}, s32[6,512]{1,0:T(8,128)S(1)}, s32[]{:T(128)}, ...), condition=%wide.region_21.22_spmd.clone, body=%wide.region_20.21_spmd.clone.sunk | while | flops 67764232 | bytes 596117 | solution.py:169
  133.2 2.1 %fusion.198 = f32[64,1024]{1,0:T(8,128)} fusion(s32[512]{0:T(512)S(1)} %bitcast.164, f32[64,1024]{1,0:T(8,128)} %get-tuple-element.1281, bf16[64,3072]{1,0:T(8,128)(2,1)} %get-tuple-element.1290, s32[]{:T(128)S(6)} %select_n.137, pred[]{:T(512)S(6)} %compare.14), kind=kOutput, calls=%fused_computation.96.clone.1 | convolution fusion | flops 67764224 | bytes 591877 | tf_op jit(solution)/shard_map/while/body/eval_jaxpr/dot_general | solution.py:165
  135.3 2.3 %fusion.198 = f32[64,1024]{1,0:T(8,128)} fusion(s32[512]{0:T(512)S(1)} %bitcast.164, f32[64,1024]{1,0:T(8,128)} %get-tuple-element.1281, bf16[64,3072]{1,0:T(8,128)(2,1)} %get-tuple-element.1290, s32[]{:T(128)S(6)} %select_n.137, pred[]{:T(512)S(6)} %compare.14), kind=kOutput, calls=%fused_computation.96.clone.1 | convolution fusion | flops 67764224 | bytes 591877 | tf_op jit(solution)/shard_map/while/body/eval_jaxpr/dot_general | solution.py:165
  137.6 2.3 %fusion.198 = f32[64,1024]{1,0:T(8,128)} fusion(s32[512]{0:T(512)S(1)} %bitcast.164, f32[64,1024]{1,0:T(8,128)} %get-tuple-element.1281, bf16[64,3072]{1,0:T(8,128)(2,1)} %get-tuple-element.1290, s32[]{:T(128)S(6)} %select_n.137, pred[]{:T(512)S(6)} %compare.14), kind=kOutput, calls=%fused_computation.96.clone.1 | convolution fusion | flops 67764224 | bytes 591877 | tf_op jit(solution)/shard_map/while/body/eval_jaxpr/dot_general | solution.py:165
  139.9 2.3 %fusion.198 = f32[64,1024]{1,0:T(8,128)} fusion(s32[512]{0:T(512)S(1)} %bitcast.164, f32[64,1024]{1,0:T(8,128)} %get-tuple-element.1281, bf16[64,3072]{1,0:T(8,128)(2,1)} %get-tuple-element.1290, s32[]{:T(128)S(6)} %select_n.137, pred[]{:T(512)S(6)} %compare.14), kind=kOutput, calls=%fused_computation.96.clone.1 | convolution fusion | flops 67764224 | bytes 591877 | tf_op jit(solution)/shard_map/while/body/eval_jaxpr/dot_general | solution.py:165
  142.1 2.3 %fusion.198 = f32[64,1024]{1,0:T(8,128)} fusion(s32[512]{0:T(512)S(1)} %bitcast.164, f32[64,1024]{1,0:T(8,128)} %get-tuple-element.1281, bf16[64,3072]{1,0:T(8,128)(2,1)} %get-tuple-element.1290, s32[]{:T(128)S(6)} %select_n.137, pred[]{:T(512)S(6)} %compare.14), kind=kOutput, calls=%fused_computation.96.clone.1 | convolution fusion | flops 67764224 | bytes 591877 | tf_op jit(solution)/shard_map/while/body/eval_jaxpr/dot_general | solution.py:165
  144.4 2.3 %fusion.198 = f32[64,1024]{1,0:T(8,128)} fusion(s32[512]{0:T(512)S(1)} %bitcast.164, f32[64,1024]{1,0:T(8,128)} %get-tuple-element.1281, bf16[64,3072]{1,0:T(8,128)(2,1)} %get-tuple-element.1290, s32[]{:T(128)S(6)} %select_n.137, pred[]{:T(512)S(6)} %compare.14), kind=kOutput, calls=%fused_computation.96.clone.1 | convolution fusion | flops 67764224 | bytes 591877 | tf_op jit(solution)/shard_map/while/body/eval_jaxpr/dot_general | solution.py:165
  147.4 6.6 %all-to-all-start.4 = ((f32[16,1,227]{2,1,0:T(1,128)}), f32[16,1,227]{2,1,0:T(1,128)S(1)}, u32[]{:S(2)}, u32[]{:S(2)}) async-start(f32[16,1,227]{2,1,0:T(1,128)} %broadcast_in_dim.148), calls=%async_computation.4 | async-start | bytes 32768 | tf_op jit(solution)/shard_map/all_to_all | solution.py:43
  154.9 5.5 %all-to-all-done.4 = f32[16,1,227]{2,1,0:T(1,128)S(1)} async-done(((f32[16,1,227]{2,1,0:T(1,128)}), f32[16,1,227]{2,1,0:T(1,128)S(1)}, u32[]{:S(2)}, u32[]{:S(2)}) %all-to-all-start.4) | async-done | bytes 14560 | tf_op jit(solution)/shard_map/all_to_all | solution.py:43
  160.4 4.4 %all-to-all-start.1 = ((bf16[64,3,4,128]{3,0,1,2:T(8,128)(2,1)}), bf16[64,3,4,128]{3,0,1,2:T(8,128)(2,1)S(1)}, u32[]{:S(2)}, u32[]{:S(2)}) async-start(bf16[64,3,4,128]{3,0,1,2:T(8,128)(2,1)} %copy.77), calls=%async_computation.1 | async-start | bytes 393216 | tf_op jit(solution)/shard_map/all_to_all | solution.py:318
  164.8 1.9 %fusion.78 = bf16[64,3072]{1,0:T(8,128)(2,1)} fusion(bf16[64,3072]{1,0:T(8,128)(2,1)S(1)} %copy-done.2, f32[192,3072]{1,0:T(8,128)} %copy-done.1), kind=kLoop, calls=%fused_computation.120 | loop fusion | flops 589824 | bytes 1572864 | tf_op jit(solution)/shard_map/convert_element_type | solution.py:233
  166.8 3.2 %all-to-all-done.1 = bf16[64,3,4,128]{3,0,1,2:T(8,128)(2,1)S(1)} async-done(((bf16[64,3,4,128]{3,0,1,2:T(8,128)(2,1)}), bf16[64,3,4,128]{3,0,1,2:T(8,128)(2,1)S(1)}, u32[]{:S(2)}, u32[]{:S(2)}) %all-to-all-start.1) | async-done | bytes 196640 | tf_op jit(solution)/shard_map/all_to_all | solution.py:318
  170.7 7.4 %all-to-all-start.5 = ((f32[8,16,227]{2,1,0:T(8,128)}), f32[8,16,227]{2,1,0:T(8,128)S(1)}, u32[]{:S(2)}, u32[]{:S(2)}) async-start(f32[8,16,227]{2,1,0:T(8,128)} %broadcast_in_dim.150), calls=%async_computation.5 | async-start | bytes 262144 | tf_op jit(solution)/shard_map/all_to_all | solution.py:43
  178.4 4.1 %while.115 = (s32[]{:T(128)}, f32[64,1024]{1,0:T(8,128)S(1)}, bf16[64,1536]{1,0:T(8,128)(2,1)S(1)}, s32[3,512]{1,0:T(4,128)}, s32[]{:T(128)}, /*index=5*/s32[]{:T(128)}, s32[]{:T(128)}, s32[]{:T(128)}) while((s32[]{:T(128)}, f32[64,1024]{1,0:T(8,128)S(1)}, bf16[64,1536]{1,0:T(8,128)(2,1)S(1)}, s32[3,512]{1,0:T(4,128)}, ...), condition=%wide.region_23.24_spmd.clone, body=%wide.region_22.23_spmd.clone.sunk | while | flops 67764232 | bytes 596117 | solution.py:169
  (308 shorter events, 78.3 us)
Async XLA Ops:
  0.6 39.6 %copy-start = (bf16[192,64]{0,1:T(8,128)(2,1)S(1)}, bf16[192,64]{0,1:T(8,128)(2,1)}, u32[]{:S(2)}) copy-start(bf16[192,64]{0,1:T(8,128)(2,1)} %param.39) | copy-start | bytes 73732
  2.1 5.0 %copy-start.14 = (pred[12,128]{1,0:T(8,128)(4,1)}, pred[12,128]{1,0:T(8,128)(4,1)S(1)}, u32[]{:S(2)}) copy-start(pred[12,128]{1,0:T(8,128)(4,1)S(1)} %compare_reduce_fusion) | copy-start | bytes 4612
  2.2 10.6 %copy-start.19 = (s32[3072]{0:T(1024)S(1)}, s32[3072]{0:T(1024)}, u32[]{:S(2)}) copy-start(s32[3072]{0:T(1024)} %param.35) | copy-start | bytes 36868
  6.4 0.6 copy-start.12
  7.0 18.1 %copy-start.24 = (bf16[64,1024]{1,0:T(8,128)(2,1)S(1)}, bf16[64,1024]{1,0:T(8,128)(2,1)}, u32[]{:S(2)}) copy-start(bf16[64,1024]{1,0:T(8,128)(2,1)} %get-tuple-element.1316) | copy-start | bytes 393220
  7.9 10.0 %all-to-all-start = ((bf16[64,3,4,128]{3,0,1,2:T(8,128)(2,1)}), bf16[64,3,4,128]{3,0,1,2:T(8,128)(2,1)S(1)}, u32[]{:S(2)}, u32[]{:S(2)}) async-start(bf16[64,3,4,128]{3,0,1,2:T(8,128)(2,1)} %copy.70), calls=%async_computation | async-start | bytes 393216 | tf_op jit(solution)/shard_map/all_to_all | solution.py:287
  17.9 10.3 %collective-permute-start.1 = (bf16[64,4,128]{2,0,1:T(8,128)(2,1)S(1)}, bf16[64,4,128]{2,0,1:T(8,128)(2,1)S(1)}, u32[]{:S(2)}, u32[]{:S(2)}) collective-permute-start(bf16[64,4,128]{2,0,1:T(8,128)(2,1)S(1)} %get-tuple-element.869), channel_id=1, source_target_pairs={{0,4},{4,8},{8,12},{12,16},{16,20},{20,24},{24,28},{28,32},{32,36}... | collective-permute-start | bytes 196616 | tf_op jit(solution)/shard_map/ppermute | solution.py:16
  23.1 5.6 %collective-permute-start = (bf16[64,4,128]{2,0,1:T(8,128)(2,1)S(1)}, bf16[64,4,128]{2,0,1:T(8,128)(2,1)S(1)}, u32[]{:S(2)}, u32[]{:S(2)}) collective-permute-start(bf16[64,4,128]{2,0,1:T(8,128)(2,1)S(1)} %get-tuple-element.868), channel_id=1, source_target_pairs={{4,0},{8,4},{12,8},{16,12},{20,16},{24,20},{28,24},{32,28},{36,32}... | collective-permute-start | bytes 196616 | tf_op jit(solution)/shard_map/ppermute | solution.py:16
  25.1 3.1 %copy-start.20 = (s32[3072]{0:T(1024)S(1)}, s32[3072]{0:T(1024)}, u32[]{:S(2)}) copy-start(s32[3072]{0:T(1024)} %param.34) | copy-start | bytes 36868
  29.0 11.1 %copy-start.9 = (bf16[64,3072]{1,0:T(8,128)(2,1)S(1)}, bf16[64,3072]{1,0:T(8,128)(2,1)}, u32[]{:S(2)}) copy-start(bf16[64,3072]{1,0:T(8,128)(2,1)} %param.33) | copy-start | bytes 1179652
  40.1 2.0 %copy-start.13 = (s32[6,512]{1,0:T(8,128)}, s32[6,512]{1,0:T(8,128)S(1)}, u32[]{:S(2)}) copy-start(s32[6,512]{1,0:T(8,128)S(1)} %get-tuple-element.1305) | copy-start | bytes 36868
  40.1 0.7 copy-start.25
  40.8 1.3 copy-start.3
  40.8 1.3 copy-start.16
  40.8 1.8 copy-start.21
  40.8 1.8 copy-start.23
  42.7 3.8 %copy-start.18 = (bf16[128,64]{0,1:T(8,128)(2,1)S(1)}, bf16[128,64]{0,1:T(8,128)(2,1)}, u32[]{:S(2)}) copy-start(bf16[128,64]{0,1:T(8,128)(2,1)} %param.44) | copy-start | bytes 49156
  42.7 3.8 %copy-start.26 = (f32[64]{0:T(128)S(1)}, f32[64]{0:T(128)}, u32[]{:S(2)}) copy-start(f32[64]{0:T(128)} %param.45) | copy-start | bytes 772
  42.7 4.0 %copy-start.17 = (bf16[64,64]{1,0:T(8,128)(2,1)S(1)}, bf16[64,64]{1,0:T(8,128)(2,1)}, u32[]{:S(2)}) copy-start(bf16[64,64]{1,0:T(8,128)(2,1)} %param.46) | copy-start | bytes 24580
  46.4 0.9 copy-start.7
  46.4 0.9 copy-start.22
  50.8 0.8 copy-start.5
  51.6 3.0 %copy-start.2 = (bf16[64,3072]{1,0:T(8,128)(2,1)S(1)}, bf16[64,3072]{1,0:T(8,128)(2,1)}, u32[]{:S(2)}) copy-start(bf16[64,3072]{1,0:T(8,128)(2,1)} %param.38) | copy-start | bytes 1179652
  56.1 1.2 copy-start.27
  57.2 1.3 copy-start.4
  59.5 15.1 %copy-start.1 = (f32[192,3072]{1,0:T(8,128)}, f32[192,3072]{1,0:T(8,128)S(1)}, u32[]{:S(2)}) copy-start(f32[192,3072]{1,0:T(8,128)S(1)} %convolution_bitcast_fusion) | copy-start | bytes 7077892
  69.6 52.7 %all-to-all-start.2 = ((f32[8,16,227]{2,1,0:T(8,128)}), f32[8,16,227]{2,1,0:T(8,128)}, u32[]{:S(2)}, u32[]{:S(2)}) async-start(f32[8,16,227]{2,1,0:T(8,128)} %copy.81), calls=%async_computation.2 | async-start | bytes 262144 | tf_op jit(solution)/shard_map/all_to_all | solution.py:26
  117.2 36.8 %collective-permute-start.2 = (bf16[64,4,128]{2,1,0:T(4,128)(2,1)S(1)}, bf16[64,4,128]{2,1,0:T(4,128)(2,1)S(1)}, u32[]{:S(2)}, u32[]{:S(2)}) collective-permute-start(bf16[64,4,128]{2,1,0:T(4,128)(2,1)S(1)} %get-tuple-element.865), channel_id=1, source_target_pairs={{0,4},{4,8},{8,12},{12,16},{16,20},{20,24},{24,28},{28,32},{32,36}... | collective-permute-start | bytes 196616 | tf_op jit(solution)/shard_map/ppermute | solution.py:16
  120.4 33.6 %collective-permute-start.3 = (bf16[64,4,128]{2,1,0:T(4,128)(2,1)S(1)}, bf16[64,4,128]{2,1,0:T(4,128)(2,1)S(1)}, u32[]{:S(2)}, u32[]{:S(2)}) collective-permute-start(bf16[64,4,128]{2,1,0:T(4,128)(2,1)S(1)} %get-tuple-element.866), channel_id=1, source_target_pairs={{4,0},{8,4},{12,8},{16,12},{20,16},{24,20},{28,24},{32,28},{36,32}... | collective-permute-start | bytes 196616 | tf_op jit(solution)/shard_map/ppermute | solution.py:16
  123.9 22.8 %all-to-all-start.3 = ((f32[16,1,227]{2,1,0:T(1,128)}), f32[16,1,227]{2,1,0:T(1,128)S(1)}, u32[]{:S(2)}, u32[]{:S(2)}) async-start(f32[16,1,227]{2,1,0:T(1,128)} %all_to_all.25), calls=%async_computation.3 | async-start | bytes 32768 | tf_op jit(solution)/shard_map/all_to_all | solution.py:33
  146.7 31.6 %copy-start.15 = (pred[12,128]{1,0:T(8,128)(4,1)S(1)}, pred[12,128]{1,0:T(8,128)(4,1)}, u32[]{:S(2)}) copy-start(pred[12,128]{1,0:T(8,128)(4,1)} %copy-done.14) | copy-start | bytes 4612
  147.4 13.1 %all-to-all-start.4 = ((f32[16,1,227]{2,1,0:T(1,128)}), f32[16,1,227]{2,1,0:T(1,128)S(1)}, u32[]{:S(2)}, u32[]{:S(2)}) async-start(f32[16,1,227]{2,1,0:T(1,128)} %broadcast_in_dim.148), calls=%async_computation.4 | async-start | bytes 32768 | tf_op jit(solution)/shard_map/all_to_all | solution.py:43
  154.0 24.3 %copy-start.10 = (f32[64,1024]{1,0:T(8,128)S(1)}, f32[64,1024]{1,0:T(8,128)}, u32[]{:S(2)}) copy-start(f32[64,1024]{1,0:T(8,128)} %custom-call.3) | copy-start | bytes 786436
  160.4 9.6 %all-to-all-start.1 = ((bf16[64,3,4,128]{3,0,1,2:T(8,128)(2,1)}), bf16[64,3,4,128]{3,0,1,2:T(8,128)(2,1)S(1)}, u32[]{:S(2)}, u32[]{:S(2)}) async-start(bf16[64,3,4,128]{3,0,1,2:T(8,128)(2,1)} %copy.77), calls=%async_computation.1 | async-start | bytes 393216 | tf_op jit(solution)/shard_map/all_to_all | solution.py:318
  170.7 12.6 %all-to-all-start.5 = ((f32[8,16,227]{2,1,0:T(8,128)}), f32[8,16,227]{2,1,0:T(8,128)S(1)}, u32[]{:S(2)}, u32[]{:S(2)}) async-start(f32[8,16,227]{2,1,0:T(8,128)} %broadcast_in_dim.150), calls=%async_computation.5 | async-start | bytes 262144 | tf_op jit(solution)/shard_map/all_to_all | solution.py:43
  178.4 4.1 %copy-start.6 = (f32[128,1024]{1,0:T(8,128)S(1)}, f32[128,1024]{1,0:T(8,128)}, u32[]{:S(2)}) copy-start(f32[128,1024]{1,0:T(8,128)} %copy-done.5) | copy-start | bytes 1572868
  178.4 4.1 %copy-start.8 = (bf16[64,1024]{1,0:T(8,128)(2,1)S(1)}, bf16[64,1024]{1,0:T(8,128)(2,1)}, u32[]{:S(2)}) copy-start(bf16[64,1024]{1,0:T(8,128)(2,1)} %param.37) | copy-start | bytes 393220
  178.4 4.1 %copy-start.11 = (f32[64,1024]{1,0:T(8,128)S(1)}, f32[64,1024]{1,0:T(8,128)}, u32[]{:S(2)}) copy-start(f32[64,1024]{1,0:T(8,128)} %get-tuple-element.665) | copy-start | bytes 786436
where the time goes:
time: 190 us; the launch traced here: 187 us
  matrix products  82.8 us (44%)
  starting transfers between devices  48.7 us (26%)
  local copies, waits for them, and re-layouts  26.8 us (14%)
  waiting for transfers between devices  14.4 us (8%)
  other arithmetic  10.9 us (6%)
    dot_general x45, matrix products, one_block(): jnp.dot(portion, selector, precision=precision, preferred_element_type=jn...  55.1 us
    dot_general x45, matrix products, one_block(): jnp.dot(table[:, begin:begin + piece], selector, precision=precision, pre...  20 us
    all_to_all x2, starting transfers between devices, copy_for_each(): lax.all_to_all(jnp.broadcast_to(array[None], (peers, *array.shape)), axis...  14 us
    ppermute x4, starting transfers between devices, from_behind(): lax.ppermute(value, axis, [(source, source + steps) for source in range(f...  12.3 us
    all_to_all x1, starting transfers between devices, sum_in_two_steps(): return jnp.sum(lax.all_to_all(own, far, 0, 0, tiled=True), axis=0)  9.24 us
    dynamic_slice x42, local copies, waits for them, and re-layouts, one_block(): chosen = lax.dynamic_index_in_dim(blocks, number, 0, keepdims=False)  6.82 us
    all_to_all x2, waiting for transfers between devices, copy_for_each(): lax.all_to_all(jnp.broadcast_to(array[None], (peers, *array.shape)), axis...  5.54 us
    all_to_all x1, waiting for transfers between devices, on_device(): lax.all_to_all(blocks, 'sub', split_axis=2, concat_axis=2, tiled=True)  5.17 us
  transfers between devices with their start and end apart: 10, of which 4 were waited for; matrix products, arithmetic and copies ran while one was open for 37% of the time, Pallas kernels for 0%

commit v1 on v0

--- a/solution.py
+++ b/solution.py
@@ -8,6 +8,18 @@
 DOM = ("dom_0", "dom_1", "dom_2")
 DOM_SUB = ("dom_0", "dom_1", "dom_2", "sub")
 EPSILON = 1e-05
+
+
+def split_up(x, dim, count):
+    dims = x.shape
+    blocks = x.reshape(*dims[:dim], count, dims[dim] // count, *dims[dim + 1 :])
+    return jnp.moveaxis(blocks, dim, 0)
+
+
+def laid_out(tiles, dim):
+    shape = list(tiles.shape[1:])
+    shape[dim] *= tiles.shape[0]
+    return jnp.moveaxis(tiles, 0, dim).reshape(shape)
 
 
 def from_behind(value, axis, steps):
@@ -284,7 +296,14 @@
     picked = column_gather(node_state, safe_index).reshape(features, peer_count, halo_width)
     outgoing = jnp.where(live_slots[None], picked, jnp.zeros_like(picked))
     blocks = outgoing.reshape(features, 3, sub_count, halo_width)
-    across = lax.all_to_all(blocks, "sub", split_axis=2, concat_axis=2, tiled=True)
+    peers_2, index_2 = (lax.axis_size("sub"), lax.axis_index("sub"))
+    blocks_2 = split_up(blocks, 2, peers_2)
+    outs = [blocks_2[index_2]]
+    for step_2 in range(1, peers_2):
+        sent = blocks_2[index_2 ^ step_2]
+        outs.append(lax.ppermute(sent, "sub", [(i, i ^ step_2) for i in range(peers_2)]))
+    blocks_2 = jnp.stack(outs)[index_2 ^ jnp.arange(peers_2)]
+    across = laid_out(blocks_2, 2)
     upper = from_behind(across[:, 0], DOM, -1)
     lower = from_behind(across[:, 2], DOM, 1)
     ghost_rows = jnp.stack([upper, across[:, 1], lower], axis=1).reshape(

time: 190 us -> 189 us (level)
    all_to_all x1 -> x0, waiting for transfers between devices: 5.17 us -> none  [on_device(): lax.all_to_all(blocks, 'sub', split_axis=2, concat_axis=2, tiled=True)]
    all_to_all x1 -> x0, starting transfers between devices: 4.83 us -> none  [on_device(): lax.all_to_all(blocks, 'sub', split_axis=2, concat_axis=2, tiled=True)]
    ppermute x0 -> x3, starting transfers between devices: none -> 4.72 us  [on_device(): lax.ppermute(sent, 'sub', [(i, i ^ step_2) for i in range(peers_2)])]
    ppermute x0 -> x3, waiting for transfers between devices: none -> 4.06 us  [on_device(): lax.ppermute(sent, 'sub', [(i, i ^ step_2) for i in range(peers_2)])]
  transfers between devices with their start and end apart: 10 -> 12, of which waited for: 4 -> 4; matrix products, arithmetic and copies ran while one was open for 37% -> 37% of each run, Pallas kernels for 0% -> 0%
where the time goes in v1:
time: 189 us; the launch traced here: 186 us
  matrix products  82.8 us (44%)
  starting transfers between devices  48.6 us (26%)
  local copies, waits for them, and re-layouts  27.1 us (14%)
  waiting for transfers between devices  12.8 us (7%)
  other arithmetic  10.9 us (6%)
    dot_general x45, matrix products, one_block(): jnp.dot(portion, selector, precision=precision, preferred_element_type=jn...  55.1 us
    dot_general x45, matrix products, one_block(): jnp.dot(table[:, begin:begin + piece], selector, precision=precision, pre...  20.1 us
    all_to_all x2, starting transfers between devices, copy_for_each(): lax.all_to_all(jnp.broadcast_to(array[None], (peers, *array.shape)), axis...  14 us
    ppermute x4, starting transfers between devices, from_behind(): lax.ppermute(value, axis, [(source, source + steps) for source in range(f...  11.8 us
    all_to_all x1, starting transfers between devices, sum_in_two_steps(): return jnp.sum(lax.all_to_all(own, far, 0, 0, tiled=True), axis=0)  9.79 us
    dynamic_slice x42, local copies, waits for them, and re-layouts, one_block(): chosen = lax.dynamic_index_in_dim(blocks, number, 0, keepdims=False)  6.82 us
    all_to_all x2, waiting for transfers between devices, copy_for_each(): lax.all_to_all(jnp.broadcast_to(array[None], (peers, *array.shape)), axis...  5.54 us
    reshape x4, local copies, waits for them, and re-layouts, packed_total(): running = total_of(jnp.concatenate([a.ravel() for a in arrays]), axis)  5.11 us
  transfers between devices with their start and end apart: 12, of which 4 were waited for; matrix products, arithmetic and copies ran while one was open for 37% of the time, Pallas kernels for 0%

profile of v1, /device:TPU:1, one launch (start us, length us, event | category | flops | bytes accessed | tf_op | source)
XLA Modules:
  0.0 185.5 jit_solution(2438313670451124174)
XLA Ops:
  2.2 4.2 %while.108 = (s32[]{:T(128)}, bf16[64,1536]{1,0:T(8,128)(2,1)S(1)}, s32[3,512]{1,0:T(4,128)S(1)}, bf16[64,1024]{1,0:T(8,128)(2,1)}, s32[]{:T(128)}, /*index=5*/s32[]{:T(128)}, s32[]{:T(128)}, s32[]{:T(128)}) while((s32[]{:T(128)}, bf16[64,1536]{1,0:T(8,128)(2,1)S(1)}, s32[3,512]{1,0:T(4,128)S(1)}, bf16[64,1024]{1,0:T(8,128)(2,1)}, s32[]{:T(128)}, ...), condition=%wide.region_1.2_spmd, body=%wide.region_0.1_spmd.sunk | while | flops 67665928 | bytes 202891 | solution.py:160
  2.2 1.4 fusion.171
  3.6 1.4 fusion.171
  5.0 1.4 fusion.171
  7.7 2.1 %collective-permute-start = (bf16[64,3,1,128]{3,0,1,2:T(8,128)(2,1)S(1)}, bf16[64,3,1,128]{3,0,1,2:T(8,128)(2,1)S(1)}, u32[]{:S(2)}, u32[]{:S(2)}) collective-permute-start(bf16[64,3,1,128]{3,0,1,2:T(8,128)(2,1)S(1)} %bitcast.206), channel_id=1, source_target_pairs={{0,1},{1,0},{2,3},{3,2},{4,5},{5,4},{6,7},{7,6},{8,9},{9,8},{10,11... | collective-permute-start | bytes 147464 | tf_op jit(solution)/shard_map/ppermute | solution.py:304
  9.8 2.5 %collective-permute-start.1 = (bf16[64,3,1,128]{3,0,1,2:T(8,128)(2,1)S(1)}, bf16[64,3,1,128]{3,0,1,2:T(8,128)(2,1)S(1)}, u32[]{:S(2)}, u32[]{:S(2)}) collective-permute-start(bf16[64,3,1,128]{3,0,1,2:T(8,128)(2,1)S(1)} %bitcast.207), channel_id=1, source_target_pairs={{0,2},{1,3},{2,0},{3,1},{4,6},{5,7},{6,4},{7,5},{8,10},{9,11},{10,... | collective-permute-start | bytes 147464 | tf_op jit(solution)/shard_map/ppermute | solution.py:304
  12.5 1.8 collective-permute-done.1
  14.3 2.3 %collective-permute-done.2 = bf16[64,3,1,128]{3,0,1,2:T(8,128)(2,1)S(1)} collective-permute-done((bf16[64,3,1,128]{3,0,1,2:T(8,128)(2,1)S(1)}, bf16[64,3,1,128]{3,0,1,2:T(8,128)(2,1)S(1)}, u32[]{:S(2)}, u32[]{:S(2)}) %collective-permute-start.2) | collective-permute-done | bytes 49184 | tf_op jit(solution)/shard_map/ppermute | solution.py:304
  17.2 4.3 %collective-permute-start.3 = (bf16[64,4,128]{2,0,1:T(8,128)(2,1)S(1)}, bf16[64,4,128]{2,0,1:T(8,128)(2,1)S(1)}, u32[]{:S(2)}, u32[]{:S(2)}) collective-permute-start(bf16[64,4,128]{2,0,1:T(8,128)(2,1)S(1)} %get-tuple-element.880), channel_id=1, source_target_pairs={{4,0},{8,4},{12,8},{16,12},{20,16},{24,20},{28,24},{32,28},{36,32}... | collective-permute-start | bytes 196616 | tf_op jit(solution)/shard_map/ppermute | solution.py:28
  21.5 3.1 %collective-permute-start.4 = (bf16[64,4,128]{2,0,1:T(8,128)(2,1)S(1)}, bf16[64,4,128]{2,0,1:T(8,128)(2,1)S(1)}, u32[]{:S(2)}, u32[]{:S(2)}) collective-permute-start(bf16[64,4,128]{2,0,1:T(8,128)(2,1)S(1)} %get-tuple-element.881), channel_id=1, source_target_pairs={{0,4},{4,8},{8,12},{12,16},{16,20},{20,24},{24,28},{28,32},{32,36}... | collective-permute-start | bytes 196616 | tf_op jit(solution)/shard_map/ppermute | solution.py:28
  24.7 3.0 %while.110 = (s32[]{:T(128)}, bf16[64,3072]{1,0:T(8,128)(2,1)S(1)}, s32[6,512]{1,0:T(8,128)S(1)}, bf16[64,1024]{1,0:T(8,128)(2,1)S(1)}, s32[]{:T(128)}, /*index=5*/s32[]{:T(128)}, s32[]{:T(128)}, s32[]{:T(128)}) while((s32[]{:T(128)}, bf16[64,3072]{1,0:T(8,128)(2,1)S(1)}, s32[6,512]{1,0:T(8,128)S(1)}, bf16[64,1024]{1,0:T(8,128)(2,1)S(1)}, ...), condition=%wide.region_5.6_spmd, body=%wide.region_4.5_spmd.sunk | while | flops 67665928 | bytes 202891 | solution.py:160
  28.1 11.0 %while.109 = (s32[]{:T(128)}, bf16[64,3072]{1,0:T(8,128)(2,1)S(1)}, s32[6,512]{1,0:T(8,128)S(1)}, bf16[64,1024]{1,0:T(8,128)(2,1)S(1)}, bf16[64,1536]{1,0:T(8,12...) while((s32[]{:T(128)}, bf16[64,3072]{1,0:T(8,128)(2,1)S(1)}, s32[6,512]{1,0:T(8,128)S(1)}, ...), condition=%wide.region_3.4_spmd, body=%wide.region_2.3_spmd.sunk | while | flops 169248768 | bytes 1472659 | solution.py:160
  39.8 1.3 multiply_convert_fusion
  41.8 3.7 %while.112 = (s32[]{:T(128)}, f32[64,1024]{1,0:T(8,128)S(1)}, bf16[64,3072]{1,0:T(8,128)(2,1)S(1)}, s32[6,512]{1,0:T(8,128)S(1)}, s32[]{:T(128)}, /*index=5*/s32[]{:T(128)}, s32[]{:T(128)}, s32[]{:T(128)}) while((s32[]{:T(128)}, f32[64,1024]{1,0:T(8,128)S(1)}, bf16[64,3072]{1,0:T(8,128)(2,1)S(1)}, s32[6,512]{1,0:T(8,128)S(1)}, ...), condition=%wide.region_9.10_spmd.clone, body=%wide.region_8.9_spmd.clone.sunk | while | flops 67764232 | bytes 596117 | solution.py:181
  50.8 3.0 %while.111 = (s32[]{:T(128)}, f32[64,3072]{1,0:T(8,128)S(1)}, s32[6,512]{1,0:T(8,128)S(1)}, bf16[64,1024]{1,0:T(8,128)(2,1)S(1)}, s32[]{:T(128)}, /*index=5*/s32[]{:T(128)}, s32[]{:T(128)}, s32[]{:T(128)}) while((s32[]{:T(128)}, f32[64,3072]{1,0:T(8,128)S(1)}, s32[6,512]{1,0:T(8,128)S(1)}, bf16[64,1024]{1,0:T(8,128)(2,1)S(1)}, s32[]{:T(128)}, ...), condition=%wide.region_15.16_spmd, body=%wide.region_14.15_spmd.sunk | while | flops 67633160 | bytes 268427 | solution.py:160
  53.8 1.4 fusion.85
  58.6 1.4 reshape.220
  60.1 1.5 reshape.219
  61.6 1.4 reshape.218
  63.7 1.6 concatenate.18
  65.3 1.9 %reshape_reshape.17 = f32[16,8,227]{2,1,0:T(8,128)} reshape(f32[29056]{0:T(1024)} %concatenate.18) | data formatting | bytes 232448 | tf_op jit(solution)/shard_map/reshape;reshape | solution.py:33
  67.2 1.6 copy.122
  68.8 4.1 %all-to-all-start.1 = ((f32[8,16,227]{2,1,0:T(8,128)}), f32[8,16,227]{2,1,0:T(8,128)}, u32[]{:S(2)}, u32[]{:S(2)}) async-start(f32[8,16,227]{2,1,0:T(8,128)} %copy.122), calls=%async_computation.1 | async-start | bytes 262144 | tf_op jit(solution)/shard_map/all_to_all | solution.py:38
  73.9 42.4 %while.113 = (s32[]{:T(128)}, f32[64,2560]{1,0:T(8,128)S(1)}, bf16[64,3072]{1,0:T(8,128)(2,1)}, s32[6,512]{1,0:T(8,128)}, s32[]{:T(128)}, /*index=5*/s32[]{:T(128)}, s32[]{:T(128)}, s32[]{:T(128)}) while((s32[]{:T(128)}, f32[64,2560]{1,0:T(8,128)S(1)}, bf16[64,3072]{1,0:T(8,128)(2,1)}, s32[6,512]{1,0:T(8,128)}, s32[]{:T(128)}, ...), condition=%wide.region_19.20_spmd.clone, body=%wide.region_18.19_spmd.clone.sunk | while | flops 169412608 | bytes 2980005 | solution.py:181
  75.8 1.2 convolution_dynamic-update-slice_fusion.11
  77.0 1.2 convolution_dynamic-update-slice_fusion.12
  90.0 1.2 convolution_dynamic-update-slice_fusion.11
  92.4 1.2 convolution_dynamic-update-slice_fusion.13
  97.0 1.2 convolution_dynamic-update-slice_fusion.11
  99.5 1.2 convolution_dynamic-update-slice_fusion.13
  113.6 1.2 convolution_dynamic-update-slice_fusion.13
  116.5 2.4 %collective-permute-start.5 = (bf16[64,4,128]{2,1,0:T(4,128)(2,1)S(1)}, bf16[64,4,128]{2,1,0:T(4,128)(2,1)S(1)}, u32[]{:S(2)}, u32[]{:S(2)}) collective-permute-start(bf16[64,4,128]{2,1,0:T(4,128)(2,1)S(1)} %get-tuple-element.877), channel_id=1, source_target_pairs={{0,4},{4,8},{8,12},{12,16},{16,20},{20,24},{24,28},{28,32},{32,36}... | collective-permute-start | bytes 196616 | tf_op jit(solution)/shard_map/ppermute | solution.py:28
  118.9 1.9 %collective-permute-start.6 = (bf16[64,4,128]{2,1,0:T(4,128)(2,1)S(1)}, bf16[64,4,128]{2,1,0:T(4,128)(2,1)S(1)}, u32[]{:S(2)}, u32[]{:S(2)}) collective-permute-start(bf16[64,4,128]{2,1,0:T(4,128)(2,1)S(1)} %get-tuple-element.878), channel_id=1, source_target_pairs={{4,0},{8,4},{12,8},{16,12},{20,16},{24,20},{28,24},{32,28},{36,32}... | collective-permute-start | bytes 196616 | tf_op jit(solution)/shard_map/ppermute | solution.py:28
  122.4 9.8 %all-to-all-start.2 = ((f32[16,1,227]{2,1,0:T(1,128)}), f32[16,1,227]{2,1,0:T(1,128)S(1)}, u32[]{:S(2)}, u32[]{:S(2)}) async-start(f32[16,1,227]{2,1,0:T(1,128)} %all_to_all.21), calls=%async_computation.2 | async-start | bytes 32768 | tf_op jit(solution)/shard_map/all_to_all | solution.py:45
  132.2 13.6 %while.114 = (s32[]{:T(128)}, f32[64,1024]{1,0:T(8,128)}, bf16[64,3072]{1,0:T(8,128)(2,1)}, s32[6,512]{1,0:T(8,128)S(1)}, s32[]{:T(128)}, /*index=5*/s32[]{:T(128)}, s32[]{:T(128)}, s32[]{:T(128)}) while((s32[]{:T(128)}, f32[64,1024]{1,0:T(8,128)}, bf16[64,3072]{1,0:T(8,128)(2,1)}, s32[6,512]{1,0:T(8,128)S(1)}, s32[]{:T(128)}, ...), condition=%wide.region_21.22_spmd.clone, body=%wide.region_20.21_spmd.clone.sunk | while | flops 67764232 | bytes 596117 | solution.py:181
  132.2 2.1 %fusion.199 = f32[64,1024]{1,0:T(8,128)} fusion(s32[512]{0:T(512)S(1)} %bitcast.198, f32[64,1024]{1,0:T(8,128)} %get-tuple-element.1297, bf16[64,3072]{1,0:T(8,128)(2,1)} %get-tuple-element.1306, s32[]{:T(128)S(6)} %select_n.173, pred[]{:T(512)S(6)} %compare.14), kind=kOutput, calls=%fused_computation.97.clone.1 | convolution fusion | flops 67764224 | bytes 591877 | tf_op jit(solution)/shard_map/while/body/eval_jaxpr/dot_general | solution.py:177
  134.4 2.3 %fusion.199 = f32[64,1024]{1,0:T(8,128)} fusion(s32[512]{0:T(512)S(1)} %bitcast.198, f32[64,1024]{1,0:T(8,128)} %get-tuple-element.1297, bf16[64,3072]{1,0:T(8,128)(2,1)} %get-tuple-element.1306, s32[]{:T(128)S(6)} %select_n.173, pred[]{:T(512)S(6)} %compare.14), kind=kOutput, calls=%fused_computation.97.clone.1 | convolution fusion | flops 67764224 | bytes 591877 | tf_op jit(solution)/shard_map/while/body/eval_jaxpr/dot_general | solution.py:177
  136.7 2.3 %fusion.199 = f32[64,1024]{1,0:T(8,128)} fusion(s32[512]{0:T(512)S(1)} %bitcast.198, f32[64,1024]{1,0:T(8,128)} %get-tuple-element.1297, bf16[64,3072]{1,0:T(8,128)(2,1)} %get-tuple-element.1306, s32[]{:T(128)S(6)} %select_n.173, pred[]{:T(512)S(6)} %compare.14), kind=kOutput, calls=%fused_computation.97.clone.1 | convolution fusion | flops 67764224 | bytes 591877 | tf_op jit(solution)/shard_map/while/body/eval_jaxpr/dot_general | solution.py:177
  138.9 2.3 %fusion.199 = f32[64,1024]{1,0:T(8,128)} fusion(s32[512]{0:T(512)S(1)} %bitcast.198, f32[64,1024]{1,0:T(8,128)} %get-tuple-element.1297, bf16[64,3072]{1,0:T(8,128)(2,1)} %get-tuple-element.1306, s32[]{:T(128)S(6)} %select_n.173, pred[]{:T(512)S(6)} %compare.14), kind=kOutput, calls=%fused_computation.97.clone.1 | convolution fusion | flops 67764224 | bytes 591877 | tf_op jit(solution)/shard_map/while/body/eval_jaxpr/dot_general | solution.py:177
  141.2 2.3 %fusion.199 = f32[64,1024]{1,0:T(8,128)} fusion(s32[512]{0:T(512)S(1)} %bitcast.198, f32[64,1024]{1,0:T(8,128)} %get-tuple-element.1297, bf16[64,3072]{1,0:T(8,128)(2,1)} %get-tuple-element.1306, s32[]{:T(128)S(6)} %select_n.173, pred[]{:T(512)S(6)} %compare.14), kind=kOutput, calls=%fused_computation.97.clone.1 | convolution fusion | flops 67764224 | bytes 591877 | tf_op jit(solution)/shard_map/while/body/eval_jaxpr/dot_general | solution.py:177
  143.5 2.3 %fusion.199 = f32[64,1024]{1,0:T(8,128)} fusion(s32[512]{0:T(512)S(1)} %bitcast.198, f32[64,1024]{1,0:T(8,128)} %get-tuple-element.1297, bf16[64,3072]{1,0:T(8,128)(2,1)} %get-tuple-element.1306, s32[]{:T(128)S(6)} %select_n.173, pred[]{:T(512)S(6)} %compare.14), kind=kOutput, calls=%fused_computation.97.clone.1 | convolution fusion | flops 67764224 | bytes 591877 | tf_op jit(solution)/shard_map/while/body/eval_jaxpr/dot_general | solution.py:177
  146.4 6.6 %all-to-all-start.3 = ((f32[16,1,227]{2,1,0:T(1,128)}), f32[16,1,227]{2,1,0:T(1,128)S(1)}, u32[]{:S(2)}, u32[]{:S(2)}) async-start(f32[16,1,227]{2,1,0:T(1,128)} %broadcast_in_dim.149), calls=%async_computation.3 | async-start | bytes 32768 | tf_op jit(solution)/shard_map/all_to_all | solution.py:55
  154.0 5.5 %all-to-all-done.3 = f32[16,1,227]{2,1,0:T(1,128)S(1)} async-done(((f32[16,1,227]{2,1,0:T(1,128)}), f32[16,1,227]{2,1,0:T(1,128)S(1)}, u32[]{:S(2)}, u32[]{:S(2)}) %all-to-all-start.3) | async-done | bytes 14560 | tf_op jit(solution)/shard_map/all_to_all | solution.py:55
  159.5 4.2 %all-to-all-start = ((bf16[64,3,4,128]{3,0,1,2:T(8,128)(2,1)}), bf16[64,3,4,128]{3,0,1,2:T(8,128)(2,1)S(1)}, u32[]{:S(2)}, u32[]{:S(2)}) async-start(bf16[64,3,4,128]{3,0,1,2:T(8,128)(2,1)} %copy.118), calls=%async_computation | async-start | bytes 393216 | tf_op jit(solution)/shard_map/all_to_all | solution.py:337
  163.7 1.9 %fusion.78 = bf16[64,3072]{1,0:T(8,128)(2,1)} fusion(bf16[64,3072]{1,0:T(8,128)(2,1)S(1)} %copy-done.2, f32[192,3072]{1,0:T(8,128)} %copy-done.1), kind=kLoop, calls=%fused_computation.121 | loop fusion | flops 589824 | bytes 1572864 | tf_op jit(solution)/shard_map/convert_element_type | solution.py:245
  165.7 3.2 %all-to-all-done = bf16[64,3,4,128]{3,0,1,2:T(8,128)(2,1)S(1)} async-done(((bf16[64,3,4,128]{3,0,1,2:T(8,128)(2,1)}), bf16[64,3,4,128]{3,0,1,2:T(8,128)(2,1)S(1)}, u32[]{:S(2)}, u32[]{:S(2)}) %all-to-all-start) | async-done | bytes 196640 | tf_op jit(solution)/shard_map/all_to_all | solution.py:337
  169.6 7.4 %all-to-all-start.4 = ((f32[8,16,227]{2,1,0:T(8,128)}), f32[8,16,227]{2,1,0:T(8,128)S(1)}, u32[]{:S(2)}, u32[]{:S(2)}) async-start(f32[8,16,227]{2,1,0:T(8,128)} %broadcast_in_dim.151), calls=%async_computation.4 | async-start | bytes 262144 | tf_op jit(solution)/shard_map/all_to_all | solution.py:55
  177.3 4.1 %while.115 = (s32[]{:T(128)}, f32[64,1024]{1,0:T(8,128)S(1)}, bf16[64,1536]{1,0:T(8,128)(2,1)S(1)}, s32[3,512]{1,0:T(4,128)}, s32[]{:T(128)}, /*index=5*/s32[]{:T(128)}, s32[]{:T(128)}, s32[]{:T(128)}) while((s32[]{:T(128)}, f32[64,1024]{1,0:T(8,128)S(1)}, bf16[64,1536]{1,0:T(8,128)(2,1)S(1)}, s32[3,512]{1,0:T(4,128)}, ...), condition=%wide.region_23.24_spmd.clone, body=%wide.region_22.23_spmd.clone.sunk | while | flops 67764232 | bytes 596117 | solution.py:181
  (320 shorter events, 80.7 us)
Async XLA Ops:
  0.6 38.7 %copy-start = (bf16[192,64]{0,1:T(8,128)(2,1)S(1)}, bf16[192,64]{0,1:T(8,128)(2,1)}, u32[]{:S(2)}) copy-start(bf16[192,64]{0,1:T(8,128)(2,1)} %param.39) | copy-start | bytes 73732
  2.1 5.0 %copy-start.14 = (pred[12,128]{1,0:T(8,128)(4,1)}, pred[12,128]{1,0:T(8,128)(4,1)S(1)}, u32[]{:S(2)}) copy-start(pred[12,128]{1,0:T(8,128)(4,1)S(1)} %compare_reduce_fusion) | copy-start | bytes 4612
  6.4 0.6 copy-start.12
  7.0 5.4 %copy-start.19 = (s32[3072]{0:T(1024)S(1)}, s32[3072]{0:T(1024)}, u32[]{:S(2)}) copy-start(s32[3072]{0:T(1024)} %param.35) | copy-start | bytes 36868
  7.0 17.6 %copy-start.24 = (bf16[64,1024]{1,0:T(8,128)(2,1)S(1)}, bf16[64,1024]{1,0:T(8,128)(2,1)}, u32[]{:S(2)}) copy-start(bf16[64,1024]{1,0:T(8,128)(2,1)} %get-tuple-element.1337) | copy-start | bytes 393220
  7.7 4.8 %collective-permute-start = (bf16[64,3,1,128]{3,0,1,2:T(8,128)(2,1)S(1)}, bf16[64,3,1,128]{3,0,1,2:T(8,128)(2,1)S(1)}, u32[]{:S(2)}, u32[]{:S(2)}) collective-permute-start(bf16[64,3,1,128]{3,0,1,2:T(8,128)(2,1)S(1)} %bitcast.206), channel_id=1, source_target_pairs={{0,1},{1,0},{2,3},{3,2},{4,5},{5,4},{6,7},{7,6},{8,9},{9,8},{10,11... | collective-permute-start | bytes 147464 | tf_op jit(solution)/shard_map/ppermute | solution.py:304
  9.8 4.5 %collective-permute-start.1 = (bf16[64,3,1,128]{3,0,1,2:T(8,128)(2,1)S(1)}, bf16[64,3,1,128]{3,0,1,2:T(8,128)(2,1)S(1)}, u32[]{:S(2)}, u32[]{:S(2)}) collective-permute-start(bf16[64,3,1,128]{3,0,1,2:T(8,128)(2,1)S(1)} %bitcast.207), channel_id=1, source_target_pairs={{0,2},{1,3},{2,0},{3,1},{4,6},{5,7},{6,4},{7,5},{8,10},{9,11},{10,... | collective-permute-start | bytes 147464 | tf_op jit(solution)/shard_map/ppermute | solution.py:304
  12.3 4.2 %collective-permute-start.2 = (bf16[64,3,1,128]{3,0,1,2:T(8,128)(2,1)S(1)}, bf16[64,3,1,128]{3,0,1,2:T(8,128)(2,1)S(1)}, u32[]{:S(2)}, u32[]{:S(2)}) collective-permute-start(bf16[64,3,1,128]{3,0,1,2:T(8,128)(2,1)S(1)} %bitcast.208), channel_id=1, source_target_pairs={{0,3},{1,2},{2,1},{3,0},{4,7},{5,6},{6,5},{7,4},{8,11},{9,10},{10,... | collective-permute-start | bytes 147464 | tf_op jit(solution)/shard_map/ppermute | solution.py:304
  17.2 10.6 %collective-permute-start.3 = (bf16[64,4,128]{2,0,1:T(8,128)(2,1)S(1)}, bf16[64,4,128]{2,0,1:T(8,128)(2,1)S(1)}, u32[]{:S(2)}, u32[]{:S(2)}) collective-permute-start(bf16[64,4,128]{2,0,1:T(8,128)(2,1)S(1)} %get-tuple-element.880), channel_id=1, source_target_pairs={{4,0},{8,4},{12,8},{16,12},{20,16},{24,20},{28,24},{32,28},{36,32}... | collective-permute-start | bytes 196616 | tf_op jit(solution)/shard_map/ppermute | solution.py:28
  21.5 6.3 %collective-permute-start.4 = (bf16[64,4,128]{2,0,1:T(8,128)(2,1)S(1)}, bf16[64,4,128]{2,0,1:T(8,128)(2,1)S(1)}, u32[]{:S(2)}, u32[]{:S(2)}) collective-permute-start(bf16[64,4,128]{2,0,1:T(8,128)(2,1)S(1)} %get-tuple-element.881), channel_id=1, source_target_pairs={{0,4},{4,8},{8,12},{12,16},{16,20},{20,24},{24,28},{28,32},{32,36}... | collective-permute-start | bytes 196616 | tf_op jit(solution)/shard_map/ppermute | solution.py:28
  24.7 3.1 %copy-start.20 = (s32[3072]{0:T(1024)S(1)}, s32[3072]{0:T(1024)}, u32[]{:S(2)}) copy-start(s32[3072]{0:T(1024)} %param.34) | copy-start | bytes 36868
  28.1 11.1 %copy-start.9 = (bf16[64,3072]{1,0:T(8,128)(2,1)S(1)}, bf16[64,3072]{1,0:T(8,128)(2,1)}, u32[]{:S(2)}) copy-start(bf16[64,3072]{1,0:T(8,128)(2,1)} %param.33) | copy-start | bytes 1179652
  39.2 2.0 %copy-start.13 = (s32[6,512]{1,0:T(8,128)}, s32[6,512]{1,0:T(8,128)S(1)}, u32[]{:S(2)}) copy-start(s32[6,512]{1,0:T(8,128)S(1)} %get-tuple-element.1320) | copy-start | bytes 36868
  39.2 0.7 copy-start.25
  39.8 1.3 copy-start.3
  39.8 1.3 copy-start.16
  39.8 1.8 copy-start.21
  39.8 1.8 copy-start.23
  41.8 3.8 %copy-start.18 = (bf16[128,64]{0,1:T(8,128)(2,1)S(1)}, bf16[128,64]{0,1:T(8,128)(2,1)}, u32[]{:S(2)}) copy-start(bf16[128,64]{0,1:T(8,128)(2,1)} %param.44) | copy-start | bytes 49156
  41.8 3.8 %copy-start.26 = (f32[64]{0:T(128)S(1)}, f32[64]{0:T(128)}, u32[]{:S(2)}) copy-start(f32[64]{0:T(128)} %param.45) | copy-start | bytes 772
  41.8 4.0 %copy-start.17 = (bf16[64,64]{1,0:T(8,128)(2,1)S(1)}, bf16[64,64]{1,0:T(8,128)(2,1)}, u32[]{:S(2)}) copy-start(bf16[64,64]{1,0:T(8,128)(2,1)} %param.46) | copy-start | bytes 24580
  45.5 0.9 copy-start.7
  45.6 0.9 copy-start.22
  49.9 0.8 copy-start.5
  50.8 3.0 %copy-start.2 = (bf16[64,3072]{1,0:T(8,128)(2,1)S(1)}, bf16[64,3072]{1,0:T(8,128)(2,1)}, u32[]{:S(2)}) copy-start(bf16[64,3072]{1,0:T(8,128)(2,1)} %param.38) | copy-start | bytes 1179652
  55.2 1.2 copy-start.27
  56.4 1.3 copy-start.4
  58.6 15.3 %copy-start.1 = (f32[192,3072]{1,0:T(8,128)}, f32[192,3072]{1,0:T(8,128)S(1)}, u32[]{:S(2)}) copy-start(f32[192,3072]{1,0:T(8,128)S(1)} %convolution_bitcast_fusion) | copy-start | bytes 7077892
  68.8 52.1 %all-to-all-start.1 = ((f32[8,16,227]{2,1,0:T(8,128)}), f32[8,16,227]{2,1,0:T(8,128)}, u32[]{:S(2)}, u32[]{:S(2)}) async-start(f32[8,16,227]{2,1,0:T(8,128)} %copy.122), calls=%async_computation.1 | async-start | bytes 262144 | tf_op jit(solution)/shard_map/all_to_all | solution.py:38
  116.5 36.6 %collective-permute-start.5 = (bf16[64,4,128]{2,1,0:T(4,128)(2,1)S(1)}, bf16[64,4,128]{2,1,0:T(4,128)(2,1)S(1)}, u32[]{:S(2)}, u32[]{:S(2)}) collective-permute-start(bf16[64,4,128]{2,1,0:T(4,128)(2,1)S(1)} %get-tuple-element.877), channel_id=1, source_target_pairs={{0,4},{4,8},{8,12},{12,16},{16,20},{20,24},{24,28},{28,32},{32,36}... | collective-permute-start | bytes 196616 | tf_op jit(solution)/shard_map/ppermute | solution.py:28
  118.9 34.2 %collective-permute-start.6 = (bf16[64,4,128]{2,1,0:T(4,128)(2,1)S(1)}, bf16[64,4,128]{2,1,0:T(4,128)(2,1)S(1)}, u32[]{:S(2)}, u32[]{:S(2)}) collective-permute-start(bf16[64,4,128]{2,1,0:T(4,128)(2,1)S(1)} %get-tuple-element.878), channel_id=1, source_target_pairs={{4,0},{8,4},{12,8},{16,12},{20,16},{24,20},{28,24},{32,28},{36,32}... | collective-permute-start | bytes 196616 | tf_op jit(solution)/shard_map/ppermute | solution.py:28
  122.4 23.4 %all-to-all-start.2 = ((f32[16,1,227]{2,1,0:T(1,128)}), f32[16,1,227]{2,1,0:T(1,128)S(1)}, u32[]{:S(2)}, u32[]{:S(2)}) async-start(f32[16,1,227]{2,1,0:T(1,128)} %all_to_all.21), calls=%async_computation.2 | async-start | bytes 32768 | tf_op jit(solution)/shard_map/all_to_all | solution.py:45
  145.8 31.4 %copy-start.15 = (pred[12,128]{1,0:T(8,128)(4,1)S(1)}, pred[12,128]{1,0:T(8,128)(4,1)}, u32[]{:S(2)}) copy-start(pred[12,128]{1,0:T(8,128)(4,1)} %copy-done.14) | copy-start | bytes 4612
  146.4 13.1 %all-to-all-start.3 = ((f32[16,1,227]{2,1,0:T(1,128)}), f32[16,1,227]{2,1,0:T(1,128)S(1)}, u32[]{:S(2)}, u32[]{:S(2)}) async-start(f32[16,1,227]{2,1,0:T(1,128)} %broadcast_in_dim.149), calls=%async_computation.3 | async-start | bytes 32768 | tf_op jit(solution)/shard_map/all_to_all | solution.py:55
  153.1 24.2 %copy-start.10 = (f32[64,1024]{1,0:T(8,128)S(1)}, f32[64,1024]{1,0:T(8,128)}, u32[]{:S(2)}) copy-start(f32[64,1024]{1,0:T(8,128)} %custom-call.3) | copy-start | bytes 786436
  159.5 9.4 %all-to-all-start = ((bf16[64,3,4,128]{3,0,1,2:T(8,128)(2,1)}), bf16[64,3,4,128]{3,0,1,2:T(8,128)(2,1)S(1)}, u32[]{:S(2)}, u32[]{:S(2)}) async-start(bf16[64,3,4,128]{3,0,1,2:T(8,128)(2,1)} %copy.118), calls=%async_computation | async-start | bytes 393216 | tf_op jit(solution)/shard_map/all_to_all | solution.py:337
  169.6 12.6 %all-to-all-start.4 = ((f32[8,16,227]{2,1,0:T(8,128)}), f32[8,16,227]{2,1,0:T(8,128)S(1)}, u32[]{:S(2)}, u32[]{:S(2)}) async-start(f32[8,16,227]{2,1,0:T(8,128)} %broadcast_in_dim.151), calls=%async_computation.4 | async-start | bytes 262144 | tf_op jit(solution)/shard_map/all_to_all | solution.py:55
  177.3 4.1 %copy-start.6 = (f32[128,1024]{1,0:T(8,128)S(1)}, f32[128,1024]{1,0:T(8,128)}, u32[]{:S(2)}) copy-start(f32[128,1024]{1,0:T(8,128)} %copy-done.5) | copy-start | bytes 1572868
  177.3 4.1 %copy-start.8 = (bf16[64,1024]{1,0:T(8,128)(2,1)S(1)}, bf16[64,1024]{1,0:T(8,128)(2,1)}, u32[]{:S(2)}) copy-start(bf16[64,1024]{1,0:T(8,128)(2,1)} %param.37) | copy-start | bytes 393220
  177.3 4.1 %copy-start.11 = (f32[64,1024]{1,0:T(8,128)S(1)}, f32[64,1024]{1,0:T(8,128)}, u32[]{:S(2)}) copy-start(f32[64,1024]{1,0:T(8,128)} %get-tuple-element.665) | copy-start | bytes 786436
